TPU v7x, 32 devices: a whole 2x2x4 slice. The times are simulated.
32 devices in a mesh: dp: 4 (over x, core), expert: 8 (over z, y).
Axes of the slice: x: 2, y: 2, z: 4, core: 2. Of those that a mesh axis runs over, the one named last changes fastest.
Arguments:
- tokens: bfloat16 [1024, 6144], P('dp', 'expert'), may hold values from -6 to 6
- cotangent: bfloat16 [1024, 6144], P('dp', 'expert'), may hold values from -6 to 6
- expert_choice: int32 [1024, 2], P('dp'), may hold values from 0 to 3, all different within a row; in each aligned block of 256 rows (0 to 255, 256 to 511, ...) at most 160 rows name the same one
- gate_values: bfloat16 [1024, 2], P('dp'), may hold values from 0.099609375 to 1
- gate_weight: bfloat16 [4, 6144, 2048], P('dp', None, 'expert'), may hold values from -0.078125 to 0.078125
- up_weight: bfloat16 [4, 6144, 2048], P('dp', None, 'expert'), may hold values from -0.078125 to 0.078125
- down_weight: bfloat16 [4, 2048, 6144], P('dp', 'expert'), may hold values from -0.125 to 0.125
- shrinker: bfloat16 [4, 32, 6144], P('dp'), may hold values from -0.078125 to 0.078125
- widener: bfloat16 [4, 2, 16, 2048], P('dp', None, None, 'expert'), may hold values from -0.375 to 0.375
- squeezer: bfloat16 [4, 16, 2048], P('dp', None, 'expert'), may hold values from -0.125 to 0.125
- spreader: bfloat16 [4, 16, 6144], P('dp'), may hold values from -0.375 to 0.375
Outputs:
- token_grad: bfloat16 [1024, 6144], P('dp', 'expert')
- gate_grad: float32 [1024, 2], P('dp')
- shrinker_grad: float32 [4, 32, 6144], P('dp')
- widener_grad: float32 [4, 2, 16, 2048], P('dp', None, None, 'expert')
- squeezer_grad: float32 [4, 16, 2048], P('dp', None, 'expert')
- spreader_grad: float32 [4, 16, 6144], P('dp')
Inputs may be any that keep to these rules, and one draw needn't show every extreme that they name: `expert_choice`: each row names 2 different experts. Among the 256 tokens of one index of dp no expert is chosen more than 160 times, and some expert is chosen exactly 160 times by the tokens of some or all indices of dp.
All inputs are finite; a program needn't handle non-finite values.
Results may differ from a plain program's by a relative error of at most 0.02.
Values may be sent and summed in bfloat16 or wider, within the bound.
A program may use at most 128 MiB of HBM per device.

v0:
```python
import jax
import jax.numpy as jnp
from jax import lax
from jax.sharding import PartitionSpec as P

adapter_scale = 2.0


def product(pattern, operand_a, operand_b):
    return jnp.einsum(pattern, operand_a, operand_b, preferred_element_type=jnp.float32)


def silu_pair(gate_pre):
    logistic = jax.nn.sigmoid(gate_pre)
    return (gate_pre * logistic, logistic * (1.0 + gate_pre * (1.0 - logistic)))


def full_rows(gathered, capacity, part_width):
    n_groups = gathered.shape[0]
    n_sources = gathered.shape[1]
    ordered = gathered.reshape(n_groups, n_sources, capacity, part_width).transpose(1, 2, 0, 3)
    return ordered.reshape(n_sources * capacity, n_groups * part_width)


def local(
    tokens,
    cotangent,
    expert_choice,
    gate_values,
    gate_weight,
    up_weight,
    down_weight,
    shrinker,
    widener,
    squeezer,
    spreader,
):
    tok_rows, part_width = tokens.shape
    top_k = expert_choice.shape[1]
    low_rank = spreader.shape[1]
    n_groups = lax.axis_size("expert")
    n_experts = lax.axis_size("dp")
    capacity = tok_rows * top_k * 5 // (4 * n_experts)
    own_rows = n_experts * capacity
    flat_choice = expert_choice.reshape(-1)
    onehot = (flat_choice[:, None] == jnp.arange(n_experts, dtype=jnp.int32)[None, :]).astype(
        jnp.int32
    )
    before = jnp.cumsum(onehot, axis=0) - onehot
    slot_index = jnp.sum(before * onehot, axis=1)
    target = flat_choice * capacity + slot_index
    placing = target[None, :] == jnp.arange(own_rows, dtype=jnp.int32)[:, None]
    stacked = jnp.repeat(jnp.concatenate([tokens, cotangent], axis=1), top_k, axis=0)
    placed = jnp.dot(
        placing.astype(jnp.bfloat16), stacked, preferred_element_type=jnp.float32
    ).astype(jnp.bfloat16)
    send_x = placed[:, :part_width].reshape(n_experts, capacity * part_width)
    send_dy = placed[:, part_width:].reshape(n_experts, capacity * part_width)
    gate_flat = gate_values.reshape(-1).astype(jnp.float32)
    send_gate = (
        jnp.sum(jnp.where(placing, gate_flat[None, :], 0.0), axis=1)
        .astype(jnp.bfloat16)
        .reshape(n_experts, capacity)
    )
    recv_x, recv_dy, recv_gate = (
        lax.all_to_all(send_x, "dp", split_axis=0, concat_axis=0, tiled=True),
        lax.all_to_all(send_dy, "dp", split_axis=0, concat_axis=0, tiled=True),
        lax.all_to_all(send_gate, "dp", split_axis=0, concat_axis=0, tiled=True),
    )
    gate_rows = recv_gate.reshape(-1).astype(jnp.float32)
    gathered_x = lax.all_gather(recv_x[None], "expert", axis=0, tiled=True)
    rows_x = full_rows(gathered_x, capacity, part_width)
    shrink_local = shrinker[0]
    widen_local = widener[0]
    squeeze_local = squeezer[0]
    spread_local = spreader[0]
    lowrank_in = product("nd,rd->nr", rows_x, shrink_local).astype(jnp.bfloat16)
    gate_pre = jnp.dot(
        rows_x, gate_weight[0], preferred_element_type=jnp.float32
    ) + adapter_scale * jnp.dot(
        lowrank_in[:, :low_rank], widen_local[0], preferred_element_type=jnp.float32
    )
    up_pre = jnp.dot(
        rows_x, up_weight[0], preferred_element_type=jnp.float32
    ) + adapter_scale * jnp.dot(
        lowrank_in[:, low_rank:], widen_local[1], preferred_element_type=jnp.float32
    )
    silu_gate, silu_slope = silu_pair(gate_pre)
    activation = (silu_gate * up_pre).astype(jnp.bfloat16)
    out_part = product("rf,nf->rn", squeeze_local, activation)
    out_low = lax.psum(out_part.astype(jnp.bfloat16), "expert").astype(jnp.float32)
    gathered_dy = lax.all_gather(recv_dy[None], "expert", axis=0, tiled=True)
    rows_dy = full_rows(gathered_dy, capacity, part_width)
    back_down = product("nd,fd->nf", rows_dy, down_weight[0])
    back_low = product("rd,nd->rn", spread_local, rows_dy)
    gate_part = jnp.sum(activation.astype(jnp.float32) * back_down, axis=1)
    scaled_low = (back_low * gate_rows[None, :]).astype(jnp.bfloat16)
    act_delta = gate_rows[:, None] * back_down + adapter_scale * product(
        "rn,rf->nf", scaled_low, squeeze_local
    )
    gate_delta = (act_delta * up_pre * silu_slope).astype(jnp.bfloat16)
    up_delta = (act_delta * silu_gate).astype(jnp.bfloat16)
    back_part = jnp.concatenate(
        [
            product("rf,nf->rn", widen_local[0], gate_delta),
            product("rf,nf->rn", widen_local[1], up_delta),
        ],
        axis=0,
    )
    back_sum, gate_sum = (
        lax.psum(back_part.astype(jnp.bfloat16), "expert").astype(jnp.float32),
        lax.psum(gate_part.astype(jnp.bfloat16), "expert").astype(jnp.float32),
    )
    low_out = out_low.astype(jnp.bfloat16)
    gate_dots = gate_sum + adapter_scale * jnp.sum(low_out.astype(jnp.float32) * back_low, axis=0)
    back_in = back_sum.astype(jnp.bfloat16)
    gate_blocks = gate_weight[0].reshape(n_groups, part_width, gate_weight.shape[2])
    up_blocks = up_weight[0].reshape(n_groups, part_width, up_weight.shape[2])
    term = product("nf,kdf->knd", gate_delta, gate_blocks) + product(
        "nf,kdf->knd", up_delta, up_blocks
    )
    token_part = (
        lax.psum_scatter(
            term.reshape(1 * lax.axis_size("expert"), own_rows * part_width).astype(jnp.bfloat16),
            "expert",
            scatter_dimension=0,
            tiled=True,
        )
        .astype(jnp.float32)
        .reshape(own_rows, part_width)
    )
    shrink_cols = lax.dynamic_slice_in_dim(
        shrink_local, lax.axis_index("expert") * part_width, part_width, 1
    )
    token_part = token_part + adapter_scale * product("rn,rd->nd", back_in, shrink_cols)
    token_back, gate_back = (
        lax.all_to_all(
            token_part.reshape(n_experts, capacity * part_width).astype(jnp.bfloat16),
            "dp",
            split_axis=0,
            concat_axis=0,
            tiled=True,
        ).astype(jnp.float32),
        lax.all_to_all(
            gate_dots.reshape(n_experts, capacity).astype(jnp.bfloat16),
            "dp",
            split_axis=0,
            concat_axis=0,
            tiled=True,
        ).astype(jnp.float32),
    )
    picked = jnp.take(token_back.reshape(own_rows, part_width), target, axis=0)
    token_grad = jnp.sum(picked.reshape(tok_rows, top_k, part_width), axis=1).astype(jnp.bfloat16)
    gate_grad = jnp.take(gate_back.reshape(own_rows), target).reshape(tok_rows, top_k)
    shrinker_grad = adapter_scale * product("rn,nd->rd", back_in, rows_x)
    widener_grad = adapter_scale * jnp.stack(
        [
            product("nr,nf->rf", lowrank_in[:, :low_rank], gate_delta),
            product("nr,nf->rf", lowrank_in[:, low_rank:], up_delta),
        ]
    )
    squeezer_grad = adapter_scale * product("rn,nf->rf", scaled_low, activation)
    weighted_low = (out_low * gate_rows[None, :]).astype(jnp.bfloat16)
    spreader_grad = adapter_scale * product("rn,nd->rd", weighted_low, rows_dy)
    return (
        token_grad,
        gate_grad,
        shrinker_grad[None],
        widener_grad[None],
        squeezer_grad[None],
        spreader_grad[None],
    )


def solution(mesh):
    placed = (
        P("dp", "expert"),
        P("dp", "expert"),
        P("dp", None),
        P("dp", None),
        P("dp", None, "expert"),
        P("dp", None, "expert"),
        P("dp", "expert", None),
        P("dp", None, None),
        P("dp", None, None, "expert"),
        P("dp", None, "expert"),
        P("dp", None, None),
    )
    return jax.shard_map(
        local,
        mesh=mesh,
        in_specs=placed,
        out_specs=(
            P("dp", "expert"),
            P("dp", None),
            P("dp", None, None),
            P("dp", None, None, "expert"),
            P("dp", None, "expert"),
            P("dp", None, None),
        ),
        check_vma=False,
    )
```

profile of v0, /device:TPU:0, one launch (start us, length us, event | category | flops | bytes accessed | tf_op | source)
XLA Modules:
  0.0 964.5 jit_solution(5538377547508068036)
XLA Ops:
  13.4 4.6 reshape.230
  22.0 3.6 all_to_all.31
  26.2 9.3 reduce.14
  35.6 3.1 reshape.284
  38.7 18.9 %all_to_all.38 = bf16[4,2,61440]{2,1,0:T(2,128)(2,1)} all-to-all(bf16[4,2,61440]{2,1,0:T(2,128)(2,1)} %reshape.284), channel_id=1, replica_groups=mesh['dp'=4,'expert'=8] {'dp'}, dimensions={0} | all-to-all | bytes 1966080 | tf_op jit(solution)/shard_map/all_to_all | solution.py:67
  57.6 3.9 reshape.285
  61.6 3.7 all_to_all.32
  65.3 9.3 reduce.15
  74.6 3.2 reshape.282
  77.8 18.2 %all_to_all.39 = bf16[4,2,61440]{2,1,0:T(2,128)(2,1)} all-to-all(bf16[4,2,61440]{2,1,0:T(2,128)(2,1)} %reshape.282), channel_id=1, replica_groups=mesh['dp'=4,'expert'=8] {'dp'}, dimensions={0} | all-to-all | bytes 1966080 | tf_op jit(solution)/shard_map/all_to_all | solution.py:66
  96.0 3.9 reshape.283
  100.6 6.1 all_to_all.40
  106.8 170.5 %all-gather.5.cloned.1.call-done = bf16[32,1,122880]{2,1,0:T(2,128)(2,1)} async-done(((bf16[4,1,122880]{2,1,0:T(2,128)(2,1)}), bf16[32,1,122880]{2,1,0:T(2,128)(2,1)}) %all-gather.5.cloned.1.call-update) | async-done | bytes 7864336 | tf_op jit(solution)/shard_map/all_gather | solution.py:92
  277.3 48.0 %reduce.2 = bf16[32,122880]{1,0:T(8,128)(2,1)} reduce(bf16[32,1,122880]{2,1,0:T(2,128)(2,1)} %all-gather.5.cloned.1.call-done, bf16[]{:T(256)} %constant.69), dimensions={1}, to_apply=%all-gather.reduce_sub_computation | reduce | bytes 15728642 | tf_op jit(solution)/shard_map/all_gather | solution.py:92
  325.3 8.2 copy.75
  333.5 10.9 %copy.60 = bf16[4,160,8,768]{3,2,1,0:T(8,128)(2,1)} copy(bf16[4,160,8,768]{3,1,0,2:T(8,128)(2,1)} %bitcast.132) | data formatting | bytes 15728640 | tf_op jit(solution)/shard_map/transpose | solution.py:21
  344.4 9.1 copy.76
  353.5 5.5 convolution_bitcast_fusion
  359.0 3.7 fusion.7
  362.7 129.5 %all-gather.7.cloned.1.call-done = bf16[32,1,122880]{2,1,0:T(2,128)(2,1)} async-done(((bf16[4,1,122880]{2,1,0:T(2,128)(2,1)}), bf16[32,1,122880]{2,1,0:T(2,128)(2,1)}) %all-gather.7.cloned.1.call-update) | async-done | bytes 7864336 | tf_op jit(solution)/shard_map/all_gather | solution.py:71
  492.2 47.5 %reduce.3 = bf16[32,122880]{1,0:T(8,128)(2,1)} reduce(bf16[32,1,122880]{2,1,0:T(2,128)(2,1)} %all-gather.7.cloned.1.call-done, bf16[]{:T(256)} %constant.69), dimensions={1}, to_apply=%all-gather.1.reduce_sub_computation | reduce | bytes 15728642 | tf_op jit(solution)/shard_map/all_gather | solution.py:71
  539.6 8.2 copy.77
  547.9 10.8 %copy.63 = bf16[4,160,8,768]{3,2,1,0:T(8,128)(2,1)} copy(bf16[4,160,8,768]{3,1,0,2:T(8,128)(2,1)} %bitcast.134) | data formatting | bytes 15728640 | tf_op jit(solution)/shard_map/transpose | solution.py:21
  558.6 8.9 copy.78
  567.6 5.8 convolution_convert_fusion.1
  573.4 3.3 fusion.3
  576.7 2.9 fusion.5
  582.2 7.8 fusion.21
  590.0 11.1 %fusion.2 = bf16[1,8,640,768]{3,2,1,0:T(8,128)(2,1)} fusion(f32[640,8,768]{2,0,1:T(8,128)} %fusion.21, bf16[8,768,256]{2,1,0:T(8,128)(2,1)S(1)} %bitcast.136, bf16[640,256]{0,1:T(8,128)(2,1)S(1)} %get-tuple-element.40), kind=kOutput, calls=%fused_computation.7 | convolution fusion | flops 2021130240 | bytes 27066368 | tf_op jit(solution)/shard_map/nf,kdf->knd/dot_general | solution.py:10
  601.1 10.9 %copy.79 = bf16[1,8,640,768]{3,1,2,0:T(8,128)(2,1)} copy(bf16[1,8,640,768]{3,2,1,0:T(8,128)(2,1)} %fusion.2) | data formatting | bytes 15728640
  619.8 38.1 %all-reduce.1 = (bf16[32,640]{1,0:T(8,128)(2,1)S(1)}, bf16[16,640]{1,0:T(8,128)(2,1)S(1)}, bf16[640]{0:T(1024)(128)(2,1)}) all-reduce(bf16[32,640]{1,0:T(8,128)(2,1)} %pad_maximum_fusion.1, bf16[16,640]{1,0:T(8,128)(2,1)} %fusion.15, bf16[640]{0:T(1024)(128)(2,1)} %get-tuple-element.35), channel_id=1, replica_groups=mesh['dp'=4,'expert'=8] {'expert'}, use_global_device_ids=true, to_apply=%region_5.6 | all-reduce | flops 31360 | bytes 125440 | tf_op jit(solution)/shard_map/psum | solution.py:111
  660.6 3.8 all-to-all-start.4
  669.2 5.7 fusion
  674.9 191.6 %all-reduce.4.cloned.1.call-done = bf16[8,491520]{1,0:T(8,128)(2,1)} async-done(((bf16[8,491520]{1,0:T(8,128)(2,1)}), bf16[8,491520]{1,0:T(8,128)(2,1)}) %all-reduce.4.cloned.1.call-update) | async-done | bytes 7864336
  866.5 21.8 %fusion.9 = f32[491520]{0:T(1024)} fusion(bf16[8,491520]{1,0:T(8,128)(2,1)} %all-reduce.4.cloned.1.call-done, u32[]{:T(128)} %bitcast.28), kind=kLoop, calls=%fused_computation.16 | loop fusion | flops 491520 | bytes 2949124 | tf_op jit(solution)/shard_map/reshape | solution.py:130
  888.2 2.7 reshape.240
  891.0 3.0 add_convert_fusion.1
  894.0 3.8 convert_element_type.181
  897.8 9.3 reduce.16
  907.1 3.1 reshape.286
  910.3 4.5 all-to-all-start.3
  914.8 5.1 fusion.1
  928.5 3.9 reshape.287
  932.5 8.9 convert_reduce_fusion
  941.3 4.2 reshape.241
  945.5 4.7 gather_fusion
  950.2 3.0 gather.13
  953.3 4.2 select_reduce_fusion
  (85 shorter events, 38.0 us)
Async XLA Ops:
  7.2 566.2 %copy-start = (bf16[1,6144,256]{2,1,0:T(8,128)(2,1)S(1)}, bf16[1,6144,256]{2,1,0:T(8,128)(2,1)}, u32[]{:S(2)}) copy-start(bf16[1,6144,256]{2,1,0:T(8,128)(2,1)} %param.15) | copy-start | bytes 9437188
  7.2 270.1 %all-gather.5.cloned.1.call-start = ((), (), s32[]{:S(2)}) async-start(), calls=%async_computation.5 | async-start | bytes 17694720 | tf_op jit(solution)/shard_map/all_gather | solution.py:92
  61.6 430.6 %all-gather.7.cloned.1.call-start = ((), (), s32[]{:S(2)}) async-start(), calls=%async_computation.6 | async-start | bytes 17694720 | tf_op jit(solution)/shard_map/all_gather | solution.py:71
  77.8 22.1 %copy-start.12 = (bf16[256,2]{0,1:T(2,128)(2,1)S(1)}, bf16[256,2]{0,1:T(2,128)(2,1)}, u32[]{:S(2)}) copy-start(bf16[256,2]{0,1:T(2,128)(2,1)} %param.14) | copy-start | bytes 3076
  99.9 766.5 %all-reduce.4.cloned.1.call-start = ((), (), s32[]{:S(2)}) async-start(), calls=%async_computation.7 | async-start | bytes 15728640
  344.4 9.1 copy-start.8
  344.4 14.6 %copy-start.13 = (bf16[1,256,6144]{2,1,0:T(8,128)(2,1)S(1)}, bf16[1,256,6144]{2,1,0:T(8,128)(2,1)}, u32[]{:S(2)}) copy-start(bf16[1,256,6144]{2,1,0:T(8,128)(2,1)} %param.17) | copy-start | bytes 9437188
  353.5 5.5 copy-start.1
  558.6 8.9 copy-start.7
  567.6 5.8 copy-start.2
  573.4 3.3 copy-start.3
  576.7 3.0 copy-start.9
  576.7 3.3 copy-start.6
  576.7 3.3 copy-start.10
  582.2 7.8 copy-start.4
  582.2 7.8 copy-start.5
  612.0 1.9 copy-start.14
  660.6 249.7 %all-to-all-start.4 = ((bf16[4,1,160]{2,1,0:T(2,128)(2,1)}), bf16[4,1,160]{2,1,0:T(2,128)(2,1)}, u32[]{:S(2)}, u32[]{:S(2)}) async-start(bf16[4,1,160]{2,1,0:T(2,128)(2,1)} %convert_element_type.182), calls=%async_computation.4 | async-start | bytes 8192 | tf_op jit(solution)/shard_map/all_to_all | solution.py:144
  910.3 18.3 %all-to-all-start.3 = ((bf16[4,2,61440]{2,1,0:T(2,128)(2,1)}), bf16[4,2,61440]{2,1,0:T(2,128)(2,1)}, u32[]{:S(2)}, u32[]{:S(2)}) async-start(bf16[4,2,61440]{2,1,0:T(2,128)(2,1)} %reshape.286), calls=%async_computation.3 | async-start | bytes 1966080 | tf_op jit(solution)/shard_map/all_to_all | solution.py:137
  914.8 5.9 copy-start.11
Sparse Core Ops, SparseCore 0:
  61.7 215.5 all-gather.4
  279.5 212.6 all-gather.6
  612.1 254.3 all-reduce.3
where the time goes:
time: 975 us; the launch traced here: 964 us
  waiting for transfers between devices  493 us (51%)
  other arithmetic  167 us (17%)
  local copies, waits for them, and re-layouts  132 us (14%)
  blocking collectives  81.3 us (8%)
  matrix products  67.1 us (7%)
  between operations  14.5 us (1%)
    unnamed x4, waiting for transfers between devices  192 us
    all_gather x1, waiting for transfers between devices, local(): gathered_dy = lax.all_gather(recv_dy[None], 'expert', axis=0, tiled=True)  171 us
    all_gather x1, waiting for transfers between devices, local(): gathered_x = lax.all_gather(recv_x[None], 'expert', axis=0, tiled=True)  130 us
    unnamed x44, local copies, waits for them, and re-layouts  69.8 us
    dot_general x15, matrix products, product(): jnp.einsum(pattern, operand_a, operand_b, preferred_element_type=jnp.floa...  56.2 us
    all_gather x1, other arithmetic, local(): gathered_dy = lax.all_gather(recv_dy[None], 'expert', axis=0, tiled=True)  48 us
    all_gather x1, other arithmetic, local(): gathered_x = lax.all_gather(recv_x[None], 'expert', axis=0, tiled=True)  47.5 us
    psum x1, blocking collectives, local(): lax.psum(back_part.astype(jnp.bfloat16), 'expert').astype(jnp.float32)  38.1 us
  transfers between devices with their start and end apart: 5, of which 4 were waited for; matrix products, arithmetic and copies ran while one was open for 19% of the time, Pallas kernels for 0%

commit v1 on v0

--- a/solution.py
+++ b/solution.py
@@ -89,7 +89,14 @@
     activation = (silu_gate * up_pre).astype(jnp.bfloat16)
     out_part = product("rf,nf->rn", squeeze_local, activation)
     out_low = lax.psum(out_part.astype(jnp.bfloat16), "expert").astype(jnp.float32)
-    gathered_dy = lax.all_gather(recv_dy[None], "expert", axis=0, tiled=True)
+    ring = [recv_dy[None]]
+    for hop in range(7):
+        ring.append(lax.ppermute(ring[-1], "expert", [(dev, (dev + 1) % 8) for dev in range(8)]))
+    gathered_dy = jnp.roll(
+        jnp.concatenate(ring[::-1], axis=0),
+        (lax.axis_index("expert") + 1) * ring[0].shape[0],
+        axis=0,
+    )
     rows_dy = full_rows(gathered_dy, capacity, part_width)
     back_down = product("nd,fd->nf", rows_dy, down_weight[0])
     back_low = product("rd,nd->rn", spread_local, rows_dy)

time: 975 us -> 957 us (0.982)
  local copies, waits for them, and re-layouts: 132 us -> 185 us
  other arithmetic: 167 us -> 120 us
  blocking collectives: 81.3 us -> 57 us
  starting transfers between devices: 8.42 us -> 18.4 us
    all_gather x1 -> x0, waiting for transfers between devices: 171 us -> none  [local(): gathered_dy = lax.all_gather(recv_dy[None], 'expert', axis=0, tiled=True)]
    ppermute x0 -> x7, waiting for transfers between devices: none -> 144 us  [local(): lax.ppermute(ring[-1], 'expert', [(dev, (dev + 1) % 8) for dev in range(8)])]
    all_gather x1 -> x0, other arithmetic: 48 us -> none  [local(): gathered_dy = lax.all_gather(recv_dy[None], 'expert', axis=0, tiled=True)]
    unnamed x44 -> x85, local copies, waits for them, and re-layouts: 69.8 us -> 98.7 us
    all_to_all x2 -> x0, blocking collectives: 24.3 us -> none  [the longest x1 18.2 us: local(): lax.all_to_all(send_x, 'dp', split_axis=0, concat_axis=0, tiled=True)]
    all_to_all x0 -> x2, waiting for transfers between devices: none -> 13.6 us  [the longest x1 13.6 us: local(): lax.all_to_all(send_x, 'dp', split_axis=0, concat_axis=0, tiled=True)]
    reshape x0 -> x1, local copies, waits for them, and re-layouts: none -> 11.8 us  [full_rows(): gathered.reshape(n_groups, n_sources, capacity, part_width)]
    unnamed x4 -> x3, waiting for transfers between devices: 192 us -> 191 us
  transfers between devices with their start and end apart: 5 -> 13, of which waited for: 4 -> 10; matrix products, arithmetic and copies ran while one was open for 19% -> 19% of each run, Pallas kernels for 0% -> 0%
where the time goes in v1:
time: 957 us; the launch traced here: 946 us
  waiting for transfers between devices  484 us (51%)
  local copies, waits for them, and re-layouts  185 us (19%)
  other arithmetic  120 us (13%)
  matrix products  66.8 us (7%)
  blocking collectives  57 us (6%)
  starting transfers between devices  18.4 us (2%)
  between operations  14.7 us (2%)
    unnamed x3, waiting for transfers between devices  191 us
    ppermute x7, waiting for transfers between devices, local(): lax.ppermute(ring[-1], 'expert', [(dev, (dev + 1) % 8) for dev in range(8)])  144 us
    all_gather x1, waiting for transfers between devices, local(): gathered_x = lax.all_gather(recv_x[None], 'expert', axis=0, tiled=True)  133 us
    unnamed x85, local copies, waits for them, and re-layouts  98.7 us
    dot_general x15, matrix products, product(): jnp.einsum(pattern, operand_a, operand_b, preferred_element_type=jnp.floa...  56 us
    all_gather x1, other arithmetic, local(): gathered_x = lax.all_gather(recv_x[None], 'expert', axis=0, tiled=True)  47.7 us
    psum x1, blocking collectives, local(): lax.psum(back_part.astype(jnp.bfloat16), 'expert').astype(jnp.float32)  38.1 us
    reshape x1, other arithmetic, local(): token_part = lax.psum_scatter(term.reshape(1 * lax.axis_size('expert'), o...  21.8 us
  transfers between devices with their start and end apart: 13, of which 10 were waited for; matrix products, arithmetic and copies ran while one was open for 19% of the time, Pallas kernels for 0%

profile of v1, /device:TPU:0, one launch (start us, length us, event | category | flops | bytes accessed | tf_op | source)
XLA Modules:
  0.0 945.6 jit_solution(10789231666626541868)
XLA Ops:
  13.3 4.6 reshape.230
  22.0 3.7 all_to_all.31
  26.2 9.3 reduce.13
  35.6 3.1 reshape.282
  38.7 18.9 %all_to_all.38 = bf16[4,2,61440]{2,1,0:T(2,128)(2,1)} all-to-all(bf16[4,2,61440]{2,1,0:T(2,128)(2,1)} %reshape.282), channel_id=1, replica_groups=mesh['dp'=4,'expert'=8] {'dp'}, dimensions={0} | all-to-all | bytes 1966080 | tf_op jit(solution)/shard_map/all_to_all | solution.py:67
  57.6 3.9 reshape.283
  66.7 24.7 %collective-permute-done = bf16[1,4,122880]{2,1,0:T(4,128)(2,1)S(1)} collective-permute-done((bf16[1,4,122880]{2,1,0:T(4,128)(2,1)S(1)}, bf16[1,4,122880]{2,1,0:T(4,128)(2,1)S(1)}, u32[]{:S(2)}, u32[]{:S(2)}) %collective-permute-start) | collective-permute-done | bytes 983072 | tf_op jit(solution)/shard_map/ppermute | solution.py:94
  92.4 25.5 %collective-permute-done.1 = bf16[1,4,122880]{2,1,0:T(4,128)(2,1)S(1)} collective-permute-done((bf16[1,4,122880]{2,1,0:T(4,128)(2,1)S(1)}, bf16[1,4,122880]{2,1,0:T(4,128)(2,1)S(1)}, u32[]{:S(2)}, u32[]{:S(2)}) %collective-permute-start.1) | collective-permute-done | bytes 983072 | tf_op jit(solution)/shard_map/ppermute | solution.py:94
  118.9 24.7 %collective-permute-done.2 = bf16[1,4,122880]{2,1,0:T(4,128)(2,1)S(1)} collective-permute-done((bf16[1,4,122880]{2,1,0:T(4,128)(2,1)S(1)}, bf16[1,4,122880]{2,1,0:T(4,128)(2,1)S(1)}, u32[]{:S(2)}, u32[]{:S(2)}) %collective-permute-start.2) | collective-permute-done | bytes 983072 | tf_op jit(solution)/shard_map/ppermute | solution.py:94
  144.6 23.8 %collective-permute-done.3 = bf16[1,4,122880]{2,1,0:T(4,128)(2,1)S(1)} collective-permute-done((bf16[1,4,122880]{2,1,0:T(4,128)(2,1)S(1)}, bf16[1,4,122880]{2,1,0:T(4,128)(2,1)S(1)}, u32[]{:S(2)}, u32[]{:S(2)}) %collective-permute-start.3) | collective-permute-done | bytes 983072 | tf_op jit(solution)/shard_map/ppermute | solution.py:94
  169.4 23.0 %collective-permute-done.4 = bf16[1,4,122880]{2,1,0:T(4,128)(2,1)S(1)} collective-permute-done((bf16[1,4,122880]{2,1,0:T(4,128)(2,1)S(1)}, bf16[1,4,122880]{2,1,0:T(4,128)(2,1)S(1)}, u32[]{:S(2)}, u32[]{:S(2)}) %collective-permute-start.4) | collective-permute-done | bytes 983072 | tf_op jit(solution)/shard_map/ppermute | solution.py:94
  193.3 22.2 %collective-permute-done.5 = bf16[1,4,122880]{2,1,0:T(4,128)(2,1)} collective-permute-done((bf16[1,4,122880]{2,1,0:T(4,128)(2,1)S(1)}, bf16[1,4,122880]{2,1,0:T(4,128)(2,1)}, u32[]{:S(2)}, u32[]{:S(2)}) %collective-permute-start.5) | collective-permute-done | bytes 983072 | tf_op jit(solution)/shard_map/ppermute | solution.py:94
  216.7 3.2 all-to-all-start
  220.0 3.7 all_to_all.32
  223.6 9.3 reduce.14
  232.9 3.1 reshape.280
  236.1 4.2 all-to-all-start.2
  240.5 13.6 %all-to-all-done.2 = bf16[4,2,61440]{2,1,0:T(2,128)(2,1)} async-done(((bf16[4,2,61440]{2,1,0:T(2,128)(2,1)}), bf16[4,2,61440]{2,1,0:T(2,128)(2,1)}, u32[]{:S(2)}, u32[]{:S(2)}) %all-to-all-start.2) | async-done | bytes 983072 | tf_op jit(solution)/shard_map/all_to_all | solution.py:66
  254.1 3.9 reshape.281
  289.0 9.1 constant_dynamic-slice_fusion
  298.1 11.8 %reshape.263 = bf16[8,4,160,768]{3,2,1,0:T(8,128)(2,1)} reshape(bf16[8,4,122880]{2,1,0:T(4,128)(2,1)} %constant_dynamic-slice_fusion) | data formatting | bytes 15728640 | tf_op jit(solution)/shard_map/reshape | solution.py:21
  309.9 10.9 %copy.73 = bf16[4,160,8,768]{3,2,1,0:T(8,128)(2,1)} copy(bf16[4,160,8,768]{3,1,0,2:T(8,128)(2,1)} %bitcast.135) | data formatting | bytes 15728640 | tf_op jit(solution)/shard_map/transpose | solution.py:21
  320.9 9.0 copy.91
  329.9 5.5 convolution_bitcast_fusion
  340.1 133.1 %all-gather.3.cloned.1.call-done = bf16[32,1,122880]{2,1,0:T(2,128)(2,1)} async-done(((bf16[4,1,122880]{2,1,0:T(2,128)(2,1)}), bf16[32,1,122880]{2,1,0:T(2,128)(2,1)}) %all-gather.3.cloned.1.call-update) | async-done | bytes 7864336 | tf_op jit(solution)/shard_map/all_gather | solution.py:71
  473.1 47.7 %reduce.2 = bf16[32,122880]{1,0:T(8,128)(2,1)} reduce(bf16[32,1,122880]{2,1,0:T(2,128)(2,1)} %all-gather.3.cloned.1.call-done, bf16[]{:T(256)} %constant.92), dimensions={1}, to_apply=%all-gather.reduce_sub_computation | reduce | bytes 15728642 | tf_op jit(solution)/shard_map/all_gather | solution.py:71
  520.9 8.1 copy.92
  529.0 10.9 %copy.76 = bf16[4,160,8,768]{3,2,1,0:T(8,128)(2,1)} copy(bf16[4,160,8,768]{3,1,0,2:T(8,128)(2,1)} %bitcast.137) | data formatting | bytes 15728640 | tf_op jit(solution)/shard_map/transpose | solution.py:21
  539.9 9.0 copy.93
  548.9 5.8 convolution_convert_fusion.1
  563.0 7.8 fusion.21
  570.8 11.1 %fusion.2 = bf16[1,8,640,768]{3,2,1,0:T(8,128)(2,1)} fusion(f32[640,8,768]{2,0,1:T(8,128)} %fusion.21, bf16[8,768,256]{2,1,0:T(8,128)(2,1)S(1)} %bitcast.139, bf16[640,256]{0,1:T(8,128)(2,1)S(1)} %get-tuple-element.46), kind=kOutput, calls=%fused_computation.7 | convolution fusion | flops 2021130240 | bytes 27066368 | tf_op jit(solution)/shard_map/nf,kdf->knd/dot_general | solution.py:10
  581.9 11.2 %copy.94 = bf16[1,8,640,768]{3,1,2,0:T(8,128)(2,1)} copy(bf16[1,8,640,768]{3,2,1,0:T(8,128)(2,1)} %fusion.2) | data formatting | bytes 15728640
  601.0 38.1 %all-reduce.1 = (bf16[32,640]{1,0:T(8,128)(2,1)S(1)}, bf16[16,640]{1,0:T(8,128)(2,1)S(1)}, bf16[640]{0:T(1024)(128)(2,1)}) all-reduce(bf16[32,640]{1,0:T(8,128)(2,1)} %pad_maximum_fusion.1, bf16[16,640]{1,0:T(8,128)(2,1)} %fusion.15, bf16[640]{0:T(1024)(128)(2,1)} %get-tuple-element.41), channel_id=1, replica_groups=mesh['dp'=4,'expert'=8] {'expert'}, use_global_device_ids=true, to_apply=%region_5.6 | all-reduce | flops 31360 | bytes 125440 | tf_op jit(solution)/shard_map/psum | solution.py:118
  641.8 3.8 all-to-all-start.4
  650.4 5.7 fusion
  656.1 191.4 %all-reduce.4.cloned.1.call-done = bf16[8,491520]{1,0:T(8,128)(2,1)} async-done(((bf16[8,491520]{1,0:T(8,128)(2,1)}), bf16[8,491520]{1,0:T(8,128)(2,1)}) %all-reduce.4.cloned.1.call-update) | async-done | bytes 7864336
  847.5 21.8 %fusion.9 = f32[491520]{0:T(1024)} fusion(bf16[8,491520]{1,0:T(8,128)(2,1)} %all-reduce.4.cloned.1.call-done, u32[]{:T(128)} %bitcast.29), kind=kLoop, calls=%fused_computation.16 | loop fusion | flops 491520 | bytes 2949124 | tf_op jit(solution)/shard_map/reshape | solution.py:137
  875.0 3.8 convert_element_type.181
  878.8 9.3 reduce.15
  888.2 3.1 reshape.284
  891.3 4.4 all-to-all-start.3
  895.8 5.1 fusion.1
  909.5 3.9 reshape.285
  913.4 8.9 convert_reduce_fusion
  922.3 4.2 reshape.241
  926.5 4.7 gather_fusion
  934.3 4.2 select_reduce_fusion
  (141 shorter events, 98.5 us)
Async XLA Ops:
  7.2 547.5 %copy-start = (bf16[1,6144,256]{2,1,0:T(8,128)(2,1)S(1)}, bf16[1,6144,256]{2,1,0:T(8,128)(2,1)}, u32[]{:S(2)}) copy-start(bf16[1,6144,256]{2,1,0:T(8,128)(2,1)} %param.15) | copy-start | bytes 9437188
  22.0 193.6 %copy-start.25 = (bf16[256,2]{0,1:T(2,128)(2,1)S(1)}, bf16[256,2]{0,1:T(2,128)(2,1)}, u32[]{:S(2)}) copy-start(bf16[256,2]{0,1:T(2,128)(2,1)} %param.14) | copy-start | bytes 3076
  64.3 27.1 %collective-permute-start = (bf16[1,4,122880]{2,1,0:T(4,128)(2,1)S(1)}, bf16[1,4,122880]{2,1,0:T(4,128)(2,1)S(1)}, u32[]{:S(2)}, u32[]{:S(2)}) collective-permute-start(bf16[1,4,122880]{2,1,0:T(4,128)(2,1)S(1)} %bitcast.140), channel_id=1, source_target_pairs={{0,1},{1,2},{2,3},{3,4},{4,5},{5,6},{6,7},{7,0},{8,9},{9,10},{10,1... | collective-permute-start | bytes 2949128 | tf_op jit(solution)/shard_map/ppermute | solution.py:94
  91.4 0.9 copy-start.4
  92.4 25.5 %collective-permute-start.1 = (bf16[1,4,122880]{2,1,0:T(4,128)(2,1)S(1)}, bf16[1,4,122880]{2,1,0:T(4,128)(2,1)S(1)}, u32[]{:S(2)}, u32[]{:S(2)}) collective-permute-start(bf16[1,4,122880]{2,1,0:T(4,128)(2,1)S(1)} %collective-permute-done), channel_id=1, source_target_pairs={{0,1},{1,2},{2,3},{3,4},{4,5},{5,6},{6,7},{7,0},{8,9},{9,10},{10,1... | collective-permute-start | bytes 2949128 | tf_op jit(solution)/shard_map/ppermute | solution.py:94
  117.9 1.0 copy-start.6
  118.9 24.7 %collective-permute-start.2 = (bf16[1,4,122880]{2,1,0:T(4,128)(2,1)S(1)}, bf16[1,4,122880]{2,1,0:T(4,128)(2,1)S(1)}, u32[]{:S(2)}, u32[]{:S(2)}) collective-permute-start(bf16[1,4,122880]{2,1,0:T(4,128)(2,1)S(1)} %collective-permute-done.1), channel_id=1, source_target_pairs={{0,1},{1,2},{2,3},{3,4},{4,5},{5,6},{6,7},{7,0},{8,9},{9,10},{10,1... | collective-permute-start | bytes 2949128 | tf_op jit(solution)/shard_map/ppermute | solution.py:94
  143.6 1.0 copy-start.8
  144.6 23.8 %collective-permute-start.3 = (bf16[1,4,122880]{2,1,0:T(4,128)(2,1)S(1)}, bf16[1,4,122880]{2,1,0:T(4,128)(2,1)S(1)}, u32[]{:S(2)}, u32[]{:S(2)}) collective-permute-start(bf16[1,4,122880]{2,1,0:T(4,128)(2,1)S(1)} %collective-permute-done.2), channel_id=1, source_target_pairs={{0,1},{1,2},{2,3},{3,4},{4,5},{5,6},{6,7},{7,0},{8,9},{9,10},{10,1... | collective-permute-start | bytes 2949128 | tf_op jit(solution)/shard_map/ppermute | solution.py:94
  168.4 1.0 copy-start.10
  169.4 23.0 %collective-permute-start.4 = (bf16[1,4,122880]{2,1,0:T(4,128)(2,1)S(1)}, bf16[1,4,122880]{2,1,0:T(4,128)(2,1)S(1)}, u32[]{:S(2)}, u32[]{:S(2)}) collective-permute-start(bf16[1,4,122880]{2,1,0:T(4,128)(2,1)S(1)} %collective-permute-done.3), channel_id=1, source_target_pairs={{0,1},{1,2},{2,3},{3,4},{4,5},{5,6},{6,7},{7,0},{8,9},{9,10},{10,1... | collective-permute-start | bytes 2949128 | tf_op jit(solution)/shard_map/ppermute | solution.py:94
  192.4 1.0 copy-start.12
  193.3 22.2 %collective-permute-start.5 = (bf16[1,4,122880]{2,1,0:T(4,128)(2,1)S(1)}, bf16[1,4,122880]{2,1,0:T(4,128)(2,1)}, u32[]{:S(2)}, u32[]{:S(2)}) collective-permute-start(bf16[1,4,122880]{2,1,0:T(4,128)(2,1)S(1)} %collective-permute-done.4), channel_id=1, source_target_pairs={{0,1},{1,2},{2,3},{3,4},{4,5},{5,6},{6,7},{7,0},{8,9},{9,10},{10,1... | collective-permute-start | bytes 2949128 | tf_op jit(solution)/shard_map/ppermute | solution.py:94
  215.5 42.8 %collective-permute-start.6 = (bf16[1,4,122880]{2,1,0:T(4,128)(2,1)}, bf16[1,4,122880]{2,1,0:T(4,128)(2,1)}, u32[]{:S(2)}, u32[]{:S(2)}) collective-permute-start(bf16[1,4,122880]{2,1,0:T(4,128)(2,1)} %collective-permute-done.5), channel_id=1, source_target_pairs={{0,1},{1,2},{2,3},{3,4},{4,5},{5,6},{6,7},{7,0},{8,9},{9,10},{10,1... | collective-permute-start | bytes 2949128 | tf_op jit(solution)/shard_map/ppermute | solution.py:94
  216.7 19.4 %all-to-all-start = ((bf16[4,1,160]{2,1,0:T(2,128)(2,1)}), bf16[4,1,160]{2,1,0:T(2,128)(2,1)S(1)}, u32[]{:S(2)}, u32[]{:S(2)}) async-start(bf16[4,1,160]{2,1,0:T(2,128)(2,1)} %convert_element_type.180), calls=%async_computation | async-start | bytes 8192 | tf_op jit(solution)/shard_map/all_to_all | solution.py:68
  236.1 18.0 %all-to-all-start.2 = ((bf16[4,2,61440]{2,1,0:T(2,128)(2,1)}), bf16[4,2,61440]{2,1,0:T(2,128)(2,1)}, u32[]{:S(2)}, u32[]{:S(2)}) async-start(bf16[4,2,61440]{2,1,0:T(2,128)(2,1)} %reshape.280), calls=%async_computation.2 | async-start | bytes 1966080 | tf_op jit(solution)/shard_map/all_to_all | solution.py:66
  240.3 232.8 %all-gather.3.cloned.1.call-start = ((), (), s32[]{:S(2)}) async-start(), calls=%async_computation.5 | async-start | bytes 17694720 | tf_op jit(solution)/shard_map/all_gather | solution.py:71
  258.0 589.4 %all-reduce.4.cloned.1.call-start = ((), (), s32[]{:S(2)}) async-start(), calls=%async_computation.6 | async-start | bytes 15728640
  258.3 10.5 %copy-start.9 = (bf16[1,4,122880]{2,1,0:T(4,128)(2,1)S(1)}, bf16[1,4,122880]{2,1,0:T(4,128)(2,1)}, u32[]{:S(2)}) copy-start(bf16[1,4,122880]{2,1,0:T(4,128)(2,1)} %copy-done.8) | copy-start | bytes 2949124
  258.3 11.8 %copy-start.7 = (bf16[1,4,122880]{2,1,0:T(4,128)(2,1)S(1)}, bf16[1,4,122880]{2,1,0:T(4,128)(2,1)}, u32[]{:S(2)}) copy-start(bf16[1,4,122880]{2,1,0:T(4,128)(2,1)} %copy-done.6) | copy-start | bytes 2949124
  258.3 13.1 %copy-start.5 = (bf16[1,4,122880]{2,1,0:T(4,128)(2,1)S(1)}, bf16[1,4,122880]{2,1,0:T(4,128)(2,1)}, u32[]{:S(2)}) copy-start(bf16[1,4,122880]{2,1,0:T(4,128)(2,1)} %copy-done.4) | copy-start | bytes 2949124
  258.3 14.5 %copy-start.3 = (bf16[4,1,122880]{2,1,0:T(2,128)(2,1)S(1)}, bf16[4,1,122880]{2,1,0:T(2,128)(2,1)}, u32[]{:S(2)}) copy-start(bf16[4,1,122880]{2,1,0:T(2,128)(2,1)} %reshape.283) | copy-start | bytes 2949124
  266.0 14.1 %copy-start.13 = (bf16[1,4,122880]{2,1,0:T(4,128)(2,1)S(1)}, bf16[1,4,122880]{2,1,0:T(4,128)(2,1)}, u32[]{:S(2)}) copy-start(bf16[1,4,122880]{2,1,0:T(4,128)(2,1)} %copy-done.12) | copy-start | bytes 2949124
  268.8 12.7 %copy-start.11 = (bf16[1,4,122880]{2,1,0:T(4,128)(2,1)S(1)}, bf16[1,4,122880]{2,1,0:T(4,128)(2,1)}, u32[]{:S(2)}) copy-start(bf16[1,4,122880]{2,1,0:T(4,128)(2,1)} %copy-done.10) | copy-start | bytes 2949124
  320.9 9.0 copy-start.21
  320.9 14.5 %copy-start.26 = (bf16[1,256,6144]{2,1,0:T(8,128)(2,1)S(1)}, bf16[1,256,6144]{2,1,0:T(8,128)(2,1)}, u32[]{:S(2)}) copy-start(bf16[1,256,6144]{2,1,0:T(8,128)(2,1)} %param.17) | copy-start | bytes 9437188
  329.9 5.5 copy-start.1
  335.4 3.5 copy-start.23
  338.1 0.8 copy-start.17
  539.9 9.0 copy-start.20
  548.9 5.8 copy-start.2
  554.7 3.1 copy-start.14
  557.8 3.0 copy-start.22
  557.8 3.3 copy-start.18
  557.8 3.3 copy-start.19
  563.0 7.8 copy-start.15
  563.0 7.8 copy-start.16
  593.1 1.9 copy-start.27
  641.8 249.6 %all-to-all-start.4 = ((bf16[4,1,160]{2,1,0:T(2,128)(2,1)}), bf16[4,1,160]{2,1,0:T(2,128)(2,1)}, u32[]{:S(2)}, u32[]{:S(2)}) async-start(bf16[4,1,160]{2,1,0:T(2,128)(2,1)} %convert_element_type.182), calls=%async_computation.4 | async-start | bytes 8192 | tf_op jit(solution)/shard_map/all_to_all | solution.py:151
  891.3 10.4 %copy-start.24 = (s32[1024]{0:T(1024)S(1)}, s32[1024]{0:T(1024)}, u32[]{:S(2)}) copy-start(s32[1024]{0:T(1024)} %pad_clamp_fusion) | copy-start | bytes 12292
  891.3 18.2 %all-to-all-start.3 = ((bf16[4,2,61440]{2,1,0:T(2,128)(2,1)}), bf16[4,2,61440]{2,1,0:T(2,128)(2,1)}, u32[]{:S(2)}, u32[]{:S(2)}) async-start(bf16[4,2,61440]{2,1,0:T(2,128)(2,1)} %reshape.284), calls=%async_computation.3 | async-start | bytes 1966080 | tf_op jit(solution)/shard_map/all_to_all | solution.py:144
Sparse Core Ops, SparseCore 0:
  258.2 214.9 all-gather.2
  593.2 254.1 all-reduce.3
